TPU v7x, 256 devices: a whole 4x4x8 slice. The times are simulated.
256 devices in a mesh: af: 4 (over y), sa: 64 (over z, x, core).
Axes of the slice: x: 4, y: 4, z: 8, core: 2. Of those that a mesh axis runs over, the one named last changes fastest.
Arguments:
- data_real: bfloat16 [64, 512, 512], P('af', 'sa'), may hold values from -0.5 to 0.5
- data_imaginary: bfloat16 [64, 512, 512], P('af', 'sa'), may hold values from -0.5 to 0.5
- wavelet_real: float32 [64], P('af'), may hold values from -2.5 to 2.5
- wavelet_imaginary: float32 [64], P('af'), may hold values from -2.5 to 2.5
- primaries_real: float32 [64, 512, 512], P('af', 'sa'), may hold values from -3 to 3
- primaries_imaginary: float32 [64, 512, 512], P('af', 'sa'), may hold values from -3 to 3
Outputs:
- updated_real: float32 [64, 512, 512], P('af', 'sa')
- updated_imaginary: float32 [64, 512, 512], P('af', 'sa')
- misfit: float32 [2], replicated
All inputs are finite; a program needn't handle non-finite values.
Results may differ from a plain program's by a relative error of at most 0.0018.
Values may be sent and summed in bfloat16 or wider, within the bound.
A program may use at most 64 MiB of HBM per device.

v0:
```python
import math
import jax
import jax.numpy as jnp
from jax import lax
from jax.sharding import Mesh
from jax.sharding import PartitionSpec as P

N = 512
F = 64
ITERS = 2
SA = ("sa_0", "sa_1", "sa_2")
AF_SA = ("af", "sa_0", "sa_1", "sa_2")
STEP_LENGTH = 0.02
THRESHOLD = 0.25


def side_by_side(arrays, axis, dim, along):
    both = jnp.concatenate(arrays, axis=along)
    result, at, finished = (lax.all_gather(both, axis, axis=dim, tiled=True), 0, [])
    for a in arrays:
        finished.append(lax.slice_in_dim(result, at, at + a.shape[along], axis=along))
        at += a.shape[along]
    return tuple(finished)


def in_one_piece(arrays, axis, split_dim, concat_dim, along):
    widths = [a.shape[along] for a in arrays]
    both = jnp.concatenate(arrays, axis=along)
    result = lax.all_to_all(both, axis, split_axis=split_dim, concat_axis=concat_dim, tiled=True)
    return tuple(jnp.split(result, [sum(widths[:k]) for k in range(1, len(widths))], axis=along))


def by_axis(value, axes):
    for axis in axes:
        value = lax.psum(value, axis)
    return value


def fourier_tables(row_index, col_index):
    phase = row_index[:, None] * col_index[None, :] % F
    angle = phase.astype(jnp.float32) * (2.0 * math.pi / F)
    factor = 1.0 / math.sqrt(F)
    return (jnp.cos(angle) * factor, jnp.sin(angle) * factor)


def highest(left, right):
    return jnp.dot(left, right, precision=lax.Precision.HIGHEST, preferred_element_type=jnp.float32)


def stacked(part_real, part_imaginary):
    return jnp.concatenate(
        [part_real.astype(jnp.bfloat16), part_imaginary.astype(jnp.bfloat16)], axis=1
    )


def shrink(values):
    return values - jnp.clip(values, -THRESHOLD, THRESHOLD)


def on_device(
    data_real, data_imaginary, wavelet_real, wavelet_imaginary, primaries_real, primaries_imaginary
):
    row_count = data_real.shape[1]
    wave_real = wavelet_real[:, None, None]
    wave_imaginary = wavelet_imaginary[:, None, None]
    current_real = primaries_real
    current_imaginary = primaries_imaginary
    own_real = data_real.astype(jnp.float32)
    own_imaginary = data_imaginary.astype(jnp.float32)
    whole_real, whole_imaginary = side_by_side((data_real, data_imaginary), SA, 1, 0)
    local_sums = []
    for iteration in range(ITERS):
        left_rows = stacked(current_real, current_imaginary)
        product_real = jnp.einsum(
            "frk,fkc->frc", left_rows, whole_real, preferred_element_type=jnp.float32
        )
        product_imaginary = jnp.einsum(
            "frk,fkc->frc", left_rows, whole_imaginary, preferred_element_type=jnp.float32
        )
        forward_real = product_real[:, :row_count] - product_imaginary[:, row_count:]
        forward_imaginary = product_imaginary[:, :row_count] + product_real[:, row_count:]
        error_real = (
            own_real
            + forward_real
            - (wave_real * current_real - wave_imaginary * current_imaginary)
        )
        error_imaginary = (
            own_imaginary
            + forward_imaginary
            - (wave_real * current_imaginary + wave_imaginary * current_real)
        )
        local_sum = jnp.sum(error_real * error_real) + jnp.sum(error_imaginary * error_imaginary)
        local_sums.append(local_sum)
        error_rows = stacked(error_real, error_imaginary)
        with_real = jnp.einsum(
            "frk,fjk->frj", error_rows, whole_real, preferred_element_type=jnp.float32
        )
        with_imaginary = jnp.einsum(
            "frk,fjk->frj", error_rows, whole_imaginary, preferred_element_type=jnp.float32
        )
        back_real = with_real[:, :row_count] + with_imaginary[:, row_count:]
        back_imaginary = with_real[:, row_count:] - with_imaginary[:, :row_count]
        gradient_real = wave_real * error_real + wave_imaginary * error_imaginary - back_real
        gradient_imaginary = (
            wave_real * error_imaginary - wave_imaginary * error_real - back_imaginary
        )
        stepped_real = current_real + STEP_LENGTH * gradient_real
        stepped_imaginary = current_imaginary + STEP_LENGTH * gradient_imaginary
        trace_real, trace_imaginary = (
            lax.all_to_all(stepped_real, "af", split_axis=2, concat_axis=0, tiled=True),
            lax.all_to_all(stepped_imaginary, "af", split_axis=2, concat_axis=0, tiled=True),
        )
        block_shape = trace_real.shape
        flat_real = trace_real.reshape(F, -1)
        flat_imaginary = trace_imaginary.reshape(F, -1)
        every_index = jnp.arange(F, dtype=jnp.int32)
        cosine, sine = fourier_tables(every_index, every_index)
        time_real = highest(cosine, flat_real) - highest(sine, flat_imaginary)
        time_imaginary = highest(sine, flat_real) + highest(cosine, flat_imaginary)
        shrunk_real = shrink(time_real)
        shrunk_imaginary = shrink(time_imaginary)
        freq_real = (highest(cosine, shrunk_real) + highest(sine, shrunk_imaginary)).reshape(
            block_shape
        )
        freq_imaginary = (highest(cosine, shrunk_imaginary) - highest(sine, shrunk_real)).reshape(
            block_shape
        )
        current_real, current_imaginary = in_one_piece((freq_real, freq_imaginary), "af", 0, 2, 1)
    totals = by_axis(jnp.stack(local_sums), AF_SA)
    misfit = totals / (F * N * N)
    return (current_real, current_imaginary, misfit)


def solution(mesh):
    split = Mesh(mesh.devices.reshape(mesh.shape["af"], 8, 4, 2), ("af", "sa_0", "sa_1", "sa_2"))
    in_specs = (
        P("af", SA, None),
        P("af", SA, None),
        P("af"),
        P("af"),
        P("af", SA, None),
        P("af", SA, None),
    )
    out_specs = (P("af", SA, None), P("af", SA, None), P())
    return jax.shard_map(
        on_device, mesh=split, in_specs=in_specs, out_specs=out_specs, check_vma=False
    )
```

profile of v0, /device:TPU:1, one launch (start us, length us, event | category | flops | bytes accessed | tf_op | source)
XLA Modules:
  0.0 275.2 jit_solution(14884716040026939522)
XLA Ops:
  7.2 1.7 pad_maximum_fusion.3
  8.9 1.0 convert_element_type.66
  9.9 1.0 convert_element_type.67
  11.0 110.2 %all-gather.2.cloned.1.call-done = bf16[32,512,512]{2,1,0:T(8,128)(2,1)} async-done(((bf16[32,8,512]{2,1,0:T(8,128)(2,1)}), bf16[32,512,512]{2,1,0:T(8,128)(2,1)}) %all-gather.2.cloned.1.call-update) | async-done | bytes 16777232 | tf_op jit(solution)/shard_map/all_gather | solution.py:19
  121.1 4.7 %fusion.6 = f32[16,16,512]{2,1,0:T(8,128)S(1)} fusion(bf16[32,512,512]{2,1,0:T(8,128)(2,1)} %all-gather.2.cloned.1.call-done, bf16[16,8,512]{2,1,0:T(8,128)(2,1)S(1)} %convert_element_type.67, bf16[16,8,512]{2,1,0:T(8,128)(2,1)S(1)} %convert_element_type.66), kind=kOutput, calls=%fused_computation.6 | convolution fusion | flops 134742016 | bytes 9175040 | tf_op jit(solution)/shard_map/frk,fkc->frc/dot_general | solution.py:77
  125.9 5.3 %fusion.14 = f32[16,16,512]{2,1,0:T(8,128)S(1)} fusion(bf16[32,512,512]{2,1,0:T(8,128)(2,1)} %all-gather.2.cloned.1.call-done, bf16[16,8,512]{2,1,0:T(8,128)(2,1)S(1)} %convert_element_type.67, bf16[16,8,512]{2,1,0:T(8,128)(2,1)S(1)} %convert_element_type.66), kind=kOutput, calls=%fused_computation.14 | convolution fusion | flops 134742016 | bytes 9175040 | tf_op jit(solution)/shard_map/frk,fkc->frc/dot_general | solution.py:74
  131.2 0.8 multiply_reduce_fusion.3
  132.1 2.3 fusion.4
  134.4 2.3 fusion.12
  136.9 0.8 copy.26
  137.8 1.5 reshape.44
  139.2 4.0 %all-to-all-start = ((f32[4,1,16384]{2,1,0:T(1,128)}), f32[4,1,16384]{2,1,0:T(1,128)S(1)}, u32[]{:S(2)}, u32[]{:S(2)}) async-start(f32[4,1,16384]{2,1,0:T(1,128)} %reshape.44), calls=%async_computation | async-start | bytes 524288 | tf_op jit(solution)/shard_map/all_to_all | solution.py:110
  143.2 0.8 copy.28
  144.0 1.5 reshape.46
  145.5 3.6 %all-to-all-done = f32[4,1,16384]{2,1,0:T(1,128)S(1)} async-done(((f32[4,1,16384]{2,1,0:T(1,128)}), f32[4,1,16384]{2,1,0:T(1,128)S(1)}, u32[]{:S(2)}, u32[]{:S(2)}) %all-to-all-start) | async-done | bytes 262176 | tf_op jit(solution)/shard_map/all_to_all | solution.py:110
  149.1 3.6 %all-to-all-start.1 = ((f32[4,1,16384]{2,1,0:T(1,128)}), f32[4,1,16384]{2,1,0:T(1,128)S(1)}, u32[]{:S(2)}, u32[]{:S(2)}) async-start(f32[4,1,16384]{2,1,0:T(1,128)} %reshape.46), calls=%async_computation.1 | async-start | bytes 524288 | tf_op jit(solution)/shard_map/all_to_all | solution.py:111
  152.7 0.5 broadcast.92
  153.3 1.4 reduce
  154.6 0.7 reshape.45
  155.3 0.6 copy.27
  155.9 0.5 fusion.32
  156.5 0.5 fusion.34
  157.0 1.0 all-to-all-done.1
  158.1 1.4 reduce.1
  159.4 0.7 reshape.47
  160.1 0.6 copy.29
  160.7 0.5 clamp_subtract_fusion.2
  161.3 0.5 clamp_subtract_fusion.3
  161.8 0.5 fusion.65
  163.3 0.5 fusion.18
  164.0 9.7 %all_to_all.96 = f32[64,16,128]{2,1,0:T(8,128)S(1)} all-to-all(f32[64,16,128]{2,1,0:T(8,128)S(1)} %pad_maximum_fusion), channel_id=1, replica_groups=mesh['af'=4,'sa_0'=8,'sa_1'=4,'sa_2'=2] {'af'}, dimensions={0} | all-to-all | bytes 1048576 | tf_op jit(solution)/shard_map/all_to_all | solution.py:29
  173.9 4.7 %fusion.2 = f32[16,16,512]{2,1,0:T(8,128)S(1)} fusion(bf16[32,512,512]{2,1,0:T(8,128)(2,1)} %all-gather.2.cloned.1.call-done, bf16[16,8,512]{2,1,0:T(8,128)(2,1)S(1)} %get-tuple-element.22, bf16[16,8,512]{2,1,0:T(8,128)(2,1)S(1)} %get-tuple-element.21), kind=kOutput, calls=%fused_computation.2 | convolution fusion | flops 134742016 | bytes 9175040 | tf_op jit(solution)/shard_map/frk,fkc->frc/dot_general | solution.py:77
  178.6 4.7 %fusion.10 = f32[16,16,512]{2,1,0:T(8,128)S(1)} fusion(bf16[32,512,512]{2,1,0:T(8,128)(2,1)} %all-gather.2.cloned.1.call-done, bf16[16,8,512]{2,1,0:T(8,128)(2,1)S(1)} %get-tuple-element.22, bf16[16,8,512]{2,1,0:T(8,128)(2,1)S(1)} %get-tuple-element.21), kind=kOutput, calls=%fused_computation.10 | convolution fusion | flops 134742016 | bytes 9175040 | tf_op jit(solution)/shard_map/frk,fkc->frc/dot_general | solution.py:74
  183.3 0.9 multiply_reduce_fusion.1
  184.3 2.3 fusion
  186.6 2.3 fusion.8
  189.1 0.8 copy.31
  190.0 1.5 reshape.48
  191.4 3.4 %all-to-all-start.3 = ((f32[4,1,16384]{2,1,0:T(1,128)}), f32[4,1,16384]{2,1,0:T(1,128)S(1)}, u32[]{:S(2)}, u32[]{:S(2)}) async-start(f32[4,1,16384]{2,1,0:T(1,128)} %reshape.48), calls=%async_computation.3 | async-start | bytes 524288 | tf_op jit(solution)/shard_map/all_to_all | solution.py:110
  194.8 0.8 copy.33
  195.7 1.5 reshape.50
  197.1 3.2 %all-to-all-done.3 = f32[4,1,16384]{2,1,0:T(1,128)S(1)} async-done(((f32[4,1,16384]{2,1,0:T(1,128)}), f32[4,1,16384]{2,1,0:T(1,128)S(1)}, u32[]{:S(2)}, u32[]{:S(2)}) %all-to-all-start.3) | async-done | bytes 262176 | tf_op jit(solution)/shard_map/all_to_all | solution.py:110
  200.3 3.7 %all-to-all-start.4 = ((f32[4,1,16384]{2,1,0:T(1,128)}), f32[4,1,16384]{2,1,0:T(1,128)S(1)}, u32[]{:S(2)}, u32[]{:S(2)}) async-start(f32[4,1,16384]{2,1,0:T(1,128)} %reshape.50), calls=%async_computation.4 | async-start | bytes 524288 | tf_op jit(solution)/shard_map/all_to_all | solution.py:111
  204.0 1.4 reduce.2
  205.4 0.7 reshape.49
  206.0 0.6 copy.32
  206.6 0.6 fusion.26
  207.2 0.5 fusion.28
  207.7 1.5 all-to-all-done.4
  209.2 1.4 reduce.3
  210.6 0.7 reshape.51
  211.3 0.6 copy.34
  211.9 0.6 clamp_subtract_fusion
  212.4 0.5 clamp_subtract_fusion.1
  213.5 0.5 fusion.62
  214.5 0.5 fusion.16
  215.2 0.8 pad_maximum_fusion.1
  216.0 3.5 %all-to-all-start.5 = ((f32[64,16,128]{2,1,0:T(8,128)}), f32[64,16,128]{2,1,0:T(8,128)S(1)}, u32[]{:S(2)}, u32[]{:S(2)}) async-start(f32[64,16,128]{2,1,0:T(8,128)} %pad_maximum_fusion.1), calls=%async_computation.5 | async-start | bytes 1048576 | tf_op jit(solution)/shard_map/all_to_all | solution.py:29
  222.0 9.3 %psum.28 = f32[2]{0:T(128)S(1)} all-reduce(f32[2]{0:T(128)S(1)} %pad_maximum_fusion.15), channel_id=1, replica_groups=mesh['af'=4,'sa_0'=8,'sa_1'=4,'sa_2'=2] {'af'}, use_global_device_ids=true, to_apply=%region_4.5 | all-reduce | flops 2 | bytes 16 | tf_op jit(solution)/shard_map/psum | solution.py:35
  231.3 12.5 %psum.29 = f32[2]{0:T(128)S(1)} all-reduce(f32[2]{0:T(128)S(1)} %psum.28), channel_id=1, replica_groups=mesh['af'=4,'sa_0'=8,'sa_1'=4,'sa_2'=2] {'sa_0'}, use_global_device_ids=true, to_apply=%region_5.6 | all-reduce | flops 2 | bytes 16 | tf_op jit(solution)/shard_map/psum | solution.py:35
  243.8 7.2 %psum.30 = f32[2]{0:T(128)S(1)} all-reduce(f32[2]{0:T(128)S(1)} %psum.29), channel_id=1, replica_groups=mesh['af'=4,'sa_0'=8,'sa_1'=4,'sa_2'=2] {'sa_1'}, use_global_device_ids=true, to_apply=%region_6.7 | all-reduce | flops 2 | bytes 16 | tf_op jit(solution)/shard_map/psum | solution.py:35
  251.1 15.4 %psum.31 = f32[2]{0:T(128)S(1)} all-reduce(f32[2]{0:T(128)S(1)} %psum.30), channel_id=1, replica_groups=mesh['af'=4,'sa_0'=8,'sa_1'=4,'sa_2'=2] {'sa_2'}, use_global_device_ids=true, to_apply=%region_7.8 | all-reduce | flops 2 | bytes 16 | tf_op jit(solution)/shard_map/psum | solution.py:35
  266.5 0.5 broadcast_multiply_fusion
  267.6 0.8 fusion.158
  (46 shorter events, 3.6 us)
Async XLA Ops:
  7.2 114.0 %all-gather.2.cloned.1.call-start = ((), (), s32[]{:S(2)}) async-start(), calls=%async_computation.6 | async-start | bytes 17039360 | tf_op jit(solution)/shard_map/all_gather | solution.py:19
  10.9 120.3 %copy-start.1 = (f32[16,8,512]{2,1,0:T(8,128)S(1)}, f32[16,8,512]{2,1,0:T(8,128)}, u32[]{:S(2)}) copy-start(f32[16,8,512]{2,1,0:T(8,128)} %param.11) | copy-start | bytes 786436
  10.9 120.3 %copy-start.2 = (f32[16,8,512]{2,1,0:T(8,128)S(1)}, f32[16,8,512]{2,1,0:T(8,128)}, u32[]{:S(2)}) copy-start(f32[16,8,512]{2,1,0:T(8,128)} %param.10) | copy-start | bytes 786436
  10.9 120.3 %copy-start.3 = (bf16[16,8,512]{2,1,0:T(8,128)(2,1)S(1)}, bf16[16,8,512]{2,1,0:T(8,128)(2,1)}, u32[]{:S(2)}) copy-start(bf16[16,8,512]{2,1,0:T(8,128)(2,1)} %param.7) | copy-start | bytes 393220
  10.9 120.3 %copy-start.4 = (bf16[16,8,512]{2,1,0:T(8,128)(2,1)S(1)}, bf16[16,8,512]{2,1,0:T(8,128)(2,1)}, u32[]{:S(2)}) copy-start(bf16[16,8,512]{2,1,0:T(8,128)(2,1)} %param.6) | copy-start | bytes 393220
  10.9 120.3 %copy-start.5 = (f32[16]{0:T(128)S(1)}, f32[16]{0:T(128)}, u32[]{:S(2)}) copy-start(f32[16]{0:T(128)} %param.9) | copy-start | bytes 196
  10.9 120.3 %copy-start.6 = (f32[16]{0:T(128)S(1)}, f32[16]{0:T(128)}, u32[]{:S(2)}) copy-start(f32[16]{0:T(128)} %param.8) | copy-start | bytes 196
  121.1 11.0 %copy-start = (bf16[32,512,512]{2,1,0:T(8,128)(2,1)S(1)}, bf16[32,512,512]{2,1,0:T(8,128)(2,1)}, u32[]{:S(2)}) copy-start(bf16[32,512,512]{2,1,0:T(8,128)(2,1)} %all-gather.2.cloned.1.call-done) | copy-start | bytes 50331652
  139.2 9.9 %all-to-all-start = ((f32[4,1,16384]{2,1,0:T(1,128)}), f32[4,1,16384]{2,1,0:T(1,128)S(1)}, u32[]{:S(2)}, u32[]{:S(2)}) async-start(f32[4,1,16384]{2,1,0:T(1,128)} %reshape.44), calls=%async_computation | async-start | bytes 524288 | tf_op jit(solution)/shard_map/all_to_all | solution.py:110
  149.1 8.9 %all-to-all-start.1 = ((f32[4,1,16384]{2,1,0:T(1,128)}), f32[4,1,16384]{2,1,0:T(1,128)S(1)}, u32[]{:S(2)}, u32[]{:S(2)}) async-start(f32[4,1,16384]{2,1,0:T(1,128)} %reshape.46), calls=%async_computation.1 | async-start | bytes 524288 | tf_op jit(solution)/shard_map/all_to_all | solution.py:111
  160.7 23.6 %slice-start = ((s8[16777216]{0:T(1024)(128)(4,1)}), s8[4194304]{0:T(1024)(128)(4,1)S(1)}, s32[]{:S(2)}) async-start(s8[16777216]{0:T(1024)(128)(4,1)} %bitcast.77), calls=%async_computation.7 | async-start | bytes 8388608
  173.7 10.6 %slice-start.1 = ((s8[16777216]{0:T(1024)(128)(4,1)}), s8[4194304]{0:T(1024)(128)(4,1)S(1)}, s32[]{:S(2)}) async-start(s8[16777216]{0:T(1024)(128)(4,1)} %bitcast.77), calls=%async_computation.8 | async-start | bytes 8388608
  173.9 10.5 %slice-start.2 = ((s8[16777216]{0:T(1024)(128)(4,1)}), s8[4194304]{0:T(1024)(128)(4,1)S(1)}, s32[]{:S(2)}) async-start(s8[16777216]{0:T(1024)(128)(4,1)} %bitcast.77), calls=%async_computation.9 | async-start | bytes 8388608
  178.6 5.7 %slice-start.3 = ((s8[16777216]{0:T(1024)(128)(4,1)}), s8[4194304]{0:T(1024)(128)(4,1)S(1)}, s32[]{:S(2)}) async-start(s8[16777216]{0:T(1024)(128)(4,1)} %bitcast.77), calls=%async_computation.10 | async-start | bytes 8388608
  191.4 8.9 %all-to-all-start.3 = ((f32[4,1,16384]{2,1,0:T(1,128)}), f32[4,1,16384]{2,1,0:T(1,128)S(1)}, u32[]{:S(2)}, u32[]{:S(2)}) async-start(f32[4,1,16384]{2,1,0:T(1,128)} %reshape.48), calls=%async_computation.3 | async-start | bytes 524288 | tf_op jit(solution)/shard_map/all_to_all | solution.py:110
  200.3 8.9 %all-to-all-start.4 = ((f32[4,1,16384]{2,1,0:T(1,128)}), f32[4,1,16384]{2,1,0:T(1,128)S(1)}, u32[]{:S(2)}, u32[]{:S(2)}) async-start(f32[4,1,16384]{2,1,0:T(1,128)} %reshape.50), calls=%async_computation.4 | async-start | bytes 524288 | tf_op jit(solution)/shard_map/all_to_all | solution.py:111
  216.0 51.0 %all-to-all-start.5 = ((f32[64,16,128]{2,1,0:T(8,128)}), f32[64,16,128]{2,1,0:T(8,128)S(1)}, u32[]{:S(2)}, u32[]{:S(2)}) async-start(f32[64,16,128]{2,1,0:T(8,128)} %pad_maximum_fusion.1), calls=%async_computation.5 | async-start | bytes 1048576 | tf_op jit(solution)/shard_map/all_to_all | solution.py:29
Sparse Core Ops, SparseCore 0:
  11.2 109.8 all-gather.1
where the time goes:
time: 276 us; the launch traced here: 275 us
  waiting for transfers between devices  120 us (43%)
  blocking collectives  54.1 us (20%)
  matrix products  37 us (13%)
  starting transfers between devices  18.2 us (7%)
  between operations  17 us (6%)
  local copies, waits for them, and re-layouts  16.5 us (6%)
  other arithmetic  12.8 us (5%)
    all_gather x1, waiting for transfers between devices, side_by_side(): lax.all_gather(both, axis, axis=dim, tiled=True)  110 us
    psum x4, blocking collectives, by_axis(): value = lax.psum(value, axis)  44.4 us
    dot_general x2, matrix products, on_device(): jnp.einsum('frk,fkc->frc', left_rows, whole_real, preferred_element_type=...  10.1 us
    all_to_all x1, blocking collectives, in_one_piece(): lax.all_to_all(both, axis, split_axis=split_dim, concat_axis=concat_dim,...  9.72 us
    dot_general x2, matrix products, on_device(): jnp.einsum('frk,fkc->frc', left_rows, whole_imaginary, preferred_element_...  9.44 us
    unnamed x34, local copies, waits for them, and re-layouts  8.78 us
    dot_general x16, matrix products, highest(): jnp.dot(left, right, precision=lax.Precision.HIGHEST, preferred_element_t...  8.37 us
    all_to_all x2, starting transfers between devices, on_device(): lax.all_to_all(stepped_real, 'af', split_axis=2, concat_axis=0, tiled=True)  7.41 us
  transfers between devices with their start and end apart: 6, of which 5 were waited for; matrix products, arithmetic and copies ran while one was open for 5% of the time, Pallas kernels for 0%

commit v1 on v0

--- a/solution.py
+++ b/solution.py
@@ -12,6 +12,22 @@
 AF_SA = ("af", "sa_0", "sa_1", "sa_2")
 STEP_LENGTH = 0.02
 THRESHOLD = 0.25
+
+
+def exchange_in_pairs(shard, axis, split, join):
+    ways, here = (lax.axis_size(axis), lax.axis_index(axis))
+    width = shard.shape[split] // ways
+    shape = list(shard.shape)
+    shape[split] = width
+    height = shape[join]
+    shape[join] = height * ways
+    full = jnp.zeros(shape, shard.dtype)
+    for mask in range(ways):
+        part = lax.dynamic_slice_in_dim(shard, (here ^ mask) * width, width, axis=split)
+        if mask:
+            part = lax.ppermute(part, axis, [(d, d ^ mask) for d in range(ways)])
+        full = lax.dynamic_update_slice_in_dim(full, part, (here ^ mask) * height, axis=join)
+    return full
 
 
 def side_by_side(arrays, axis, dim, along):
@@ -107,7 +123,7 @@
         stepped_real = current_real + STEP_LENGTH * gradient_real
         stepped_imaginary = current_imaginary + STEP_LENGTH * gradient_imaginary
         trace_real, trace_imaginary = (
-            lax.all_to_all(stepped_real, "af", split_axis=2, concat_axis=0, tiled=True),
+            exchange_in_pairs(stepped_real, "af", 2, 0),
             lax.all_to_all(stepped_imaginary, "af", split_axis=2, concat_axis=0, tiled=True),
         )
         block_shape = trace_real.shape

time: 276 us -> 267 us (0.967)
  local copies, waits for them, and re-layouts: 16.5 us -> 9.59 us
  other arithmetic: 12.8 us -> 9.97 us
    ppermute x0 -> x6, waiting for transfers between devices: none -> 11.2 us  [exchange_in_pairs(): part = lax.ppermute(part, axis, [(d, d ^ mask) for d in range(ways)])]
    ppermute x0 -> x6, starting transfers between devices: none -> 9.39 us  [exchange_in_pairs(): part = lax.ppermute(part, axis, [(d, d ^ mask) for d in range(ways)])]
    all_to_all x2 -> x0, starting transfers between devices: 7.41 us -> none  [on_device(): lax.all_to_all(stepped_real, 'af', split_axis=2, concat_axis=0, tiled=True)]
    all_to_all x2 -> x0, waiting for transfers between devices: 6.86 us -> none  [on_device(): lax.all_to_all(stepped_real, 'af', split_axis=2, concat_axis=0, tiled=True)]
    psum x4, blocking collectives: 44.4 us -> 40.1 us  [by_axis(): value = lax.psum(value, axis)]
    unnamed x34 -> x30, local copies, waits for them, and re-layouts: 8.78 us -> 4.52 us
  transfers between devices with their start and end apart: 6 -> 10, of which waited for: 5 -> 5; matrix products, arithmetic and copies ran while one was open for 5% -> 3% of each run, Pallas kernels for 0% -> 0%
where the time goes in v1:
time: 267 us
  waiting for transfers between devices  121 us (45%)
  blocking collectives  51.6 us (19%)
  matrix products  37 us (14%)
  starting transfers between devices  20 us (7%)
  between operations  17 us (6%)
  other arithmetic  9.97 us (4%)
  local copies, waits for them, and re-layouts  9.59 us (4%)
    all_gather x1, waiting for transfers between devices, side_by_side(): lax.all_gather(both, axis, axis=dim, tiled=True)  110 us
    psum x4, blocking collectives, by_axis(): value = lax.psum(value, axis)  40.1 us
    all_to_all x1, blocking collectives, in_one_piece(): lax.all_to_all(both, axis, split_axis=split_dim, concat_axis=concat_dim,...  11.5 us
    ppermute x6, waiting for transfers between devices, exchange_in_pairs(): part = lax.ppermute(part, axis, [(d, d ^ mask) for d in range(ways)])  11.2 us
    dot_general x2, matrix products, on_device(): jnp.einsum('frk,fkc->frc', left_rows, whole_real, preferred_element_type=...  10.1 us
    dot_general x2, matrix products, on_device(): jnp.einsum('frk,fkc->frc', left_rows, whole_imaginary, preferred_element_...  9.44 us
    ppermute x6, starting transfers between devices, exchange_in_pairs(): part = lax.ppermute(part, axis, [(d, d ^ mask) for d in range(ways)])  9.39 us
    dot_general x16, matrix products, highest(): jnp.dot(left, right, precision=lax.Precision.HIGHEST, preferred_element_t...  8.38 us
  transfers between devices with their start and end apart: 10, of which 5 were waited for; matrix products, arithmetic and copies ran while one was open for 3% of the time, Pallas kernels for 0%

profile of v1, /device:TPU:1, one launch (start us, length us, event | category | flops | bytes accessed | tf_op | source)
XLA Modules:
  0.0 266.6 jit_solution(15404997561926255603)
XLA Ops:
  7.2 1.7 pad_maximum_fusion.3
  8.9 1.0 convert_element_type.67
  9.9 1.0 convert_element_type.66
  11.0 110.1 %all-gather.2.cloned.1.call-done = bf16[32,512,512]{2,1,0:T(8,128)(2,1)} async-done(((bf16[32,8,512]{2,1,0:T(8,128)(2,1)}), bf16[32,512,512]{2,1,0:T(8,128)(2,1)}) %all-gather.2.cloned.1.call-update) | async-done | bytes 16777232 | tf_op jit(solution)/shard_map/all_gather | solution.py:35
  121.1 4.7 %fusion.6 = f32[16,16,512]{2,1,0:T(8,128)S(1)} fusion(bf16[32,512,512]{2,1,0:T(8,128)(2,1)} %all-gather.2.cloned.1.call-done, bf16[16,8,512]{2,1,0:T(8,128)(2,1)S(1)} %convert_element_type.67, bf16[16,8,512]{2,1,0:T(8,128)(2,1)S(1)} %convert_element_type.66), kind=kOutput, calls=%fused_computation.6 | convolution fusion | flops 134742016 | bytes 9175040 | tf_op jit(solution)/shard_map/frk,fkc->frc/dot_general | solution.py:93
  125.9 5.3 %fusion.14 = f32[16,16,512]{2,1,0:T(8,128)S(1)} fusion(bf16[32,512,512]{2,1,0:T(8,128)(2,1)} %all-gather.2.cloned.1.call-done, bf16[16,8,512]{2,1,0:T(8,128)(2,1)S(1)} %convert_element_type.67, bf16[16,8,512]{2,1,0:T(8,128)(2,1)S(1)} %convert_element_type.66), kind=kOutput, calls=%fused_computation.14 | convolution fusion | flops 134742016 | bytes 9175040 | tf_op jit(solution)/shard_map/frk,fkc->frc/dot_general | solution.py:90
  131.2 0.8 multiply_reduce_fusion.3
  132.1 2.3 fusion.4
  134.4 2.3 fusion.12
  136.7 0.2 fusion.47
  137.0 1.3 collective-permute-start
  138.3 0.8 copy.20
  139.1 1.5 reshape.42
  140.6 3.7 %all-to-all-start = ((f32[4,1,16384]{2,1,0:T(1,128)}), f32[4,1,16384]{2,1,0:T(1,128)S(1)}, u32[]{:S(2)}, u32[]{:S(2)}) async-start(f32[4,1,16384]{2,1,0:T(1,128)} %reshape.42), calls=%async_computation | async-start | bytes 524288 | tf_op jit(solution)/shard_map/all_to_all | solution.py:127
  144.3 3.0 %collective-permute-start.1 = (f32[16,8,128]{2,1,0:T(8,128)S(1)}, f32[16,8,128]{2,1,0:T(8,128)S(1)}, u32[]{:S(2)}, u32[]{:S(2)}) collective-permute-start(f32[16,8,128]{2,1,0:T(8,128)S(1)} %get-tuple-element.28), channel_id=1, source_target_pairs={{0,128},{64,192},{128,0},{192,64},{1,129},{65,193},{129,1},{193,65... | collective-permute-start | bytes 196616 | tf_op jit(solution)/shard_map/ppermute | solution.py:28
  147.3 0.9 collective-permute-start.2
  148.2 3.5 %collective-permute-done.1 = f32[16,8,128]{2,1,0:T(8,128)S(1)} collective-permute-done((f32[16,8,128]{2,1,0:T(8,128)S(1)}, f32[16,8,128]{2,1,0:T(8,128)S(1)}, u32[]{:S(2)}, u32[]{:S(2)}) %collective-permute-start.1) | collective-permute-done | bytes 65568 | tf_op jit(solution)/shard_map/ppermute | solution.py:28
  151.7 2.6 collective-permute-done.2
  154.2 0.6 broadcast.96
  154.8 1.3 reduce
  156.2 0.7 reshape.43
  156.8 0.6 copy.21
  157.4 0.5 fusion.30
  158.0 0.5 fusion.32
  158.5 0.5 clamp_subtract_fusion.2
  159.1 0.5 fusion.64
  159.6 0.5 clamp_subtract_fusion.3
  160.1 0.5 fusion.65
  160.7 0.5 fusion.18
  161.2 0.5 fusion.19
  161.8 11.5 %all_to_all.66 = f32[64,16,128]{2,1,0:T(8,128)S(1)} all-to-all(f32[64,16,128]{2,1,0:T(8,128)S(1)} %pad_maximum_fusion), channel_id=1, replica_groups=mesh['af'=4,'sa_0'=8,'sa_1'=4,'sa_2'=2] {'af'}, dimensions={0} | all-to-all | bytes 1048576 | tf_op jit(solution)/shard_map/all_to_all | solution.py:45
  173.4 4.7 %fusion.2 = f32[16,16,512]{2,1,0:T(8,128)S(1)} fusion(bf16[32,512,512]{2,1,0:T(8,128)(2,1)} %all-gather.2.cloned.1.call-done, bf16[16,8,512]{2,1,0:T(8,128)(2,1)S(1)} %get-tuple-element.22, bf16[16,8,512]{2,1,0:T(8,128)(2,1)S(1)} %get-tuple-element.21), kind=kOutput, calls=%fused_computation.2 | convolution fusion | flops 134742016 | bytes 9175040 | tf_op jit(solution)/shard_map/frk,fkc->frc/dot_general | solution.py:93
  178.2 4.7 %fusion.10 = f32[16,16,512]{2,1,0:T(8,128)S(1)} fusion(bf16[32,512,512]{2,1,0:T(8,128)(2,1)} %all-gather.2.cloned.1.call-done, bf16[16,8,512]{2,1,0:T(8,128)(2,1)S(1)} %get-tuple-element.22, bf16[16,8,512]{2,1,0:T(8,128)(2,1)S(1)} %get-tuple-element.21), kind=kOutput, calls=%fused_computation.10 | convolution fusion | flops 134742016 | bytes 9175040 | tf_op jit(solution)/shard_map/frk,fkc->frc/dot_general | solution.py:90
  182.9 0.8 multiply_reduce_fusion.1
  183.8 2.3 fusion
  186.1 2.3 fusion.8
  188.7 0.4 collective-permute-start.3
  189.1 0.8 copy.23
  189.9 1.5 reshape.44
  191.4 3.4 %all-to-all-start.2 = ((f32[4,1,16384]{2,1,0:T(1,128)}), f32[4,1,16384]{2,1,0:T(1,128)S(1)}, u32[]{:S(2)}, u32[]{:S(2)}) async-start(f32[4,1,16384]{2,1,0:T(1,128)} %reshape.44), calls=%async_computation.2 | async-start | bytes 524288 | tf_op jit(solution)/shard_map/all_to_all | solution.py:127
  194.8 2.9 %collective-permute-start.4 = (f32[16,8,128]{2,1,0:T(8,128)S(1)}, f32[16,8,128]{2,1,0:T(8,128)S(1)}, u32[]{:S(2)}, u32[]{:S(2)}) collective-permute-start(f32[16,8,128]{2,1,0:T(8,128)S(1)} %get-tuple-element.24), channel_id=1, source_target_pairs={{0,128},{64,192},{128,0},{192,64},{1,129},{65,193},{129,1},{193,65... | collective-permute-start | bytes 196616 | tf_op jit(solution)/shard_map/ppermute | solution.py:28
  197.7 0.9 collective-permute-start.5
  198.7 2.3 collective-permute-done.4
  201.0 2.8 %collective-permute-done.5 = f32[16,8,128]{2,1,0:T(8,128)S(1)} collective-permute-done((f32[16,8,128]{2,1,0:T(8,128)S(1)}, f32[16,8,128]{2,1,0:T(8,128)S(1)}, u32[]{:S(2)}, u32[]{:S(2)}) %collective-permute-start.5) | collective-permute-done | bytes 65568 | tf_op jit(solution)/shard_map/ppermute | solution.py:28
  203.8 1.3 reduce.1
  205.2 0.7 reshape.45
  205.9 0.6 copy.24
  206.5 0.6 fusion.24
  207.0 0.5 fusion.26
  207.6 0.5 clamp_subtract_fusion
  208.1 0.5 fusion.62
  208.6 0.5 clamp_subtract_fusion.1
  209.2 0.5 fusion.63
  209.7 0.5 fusion.16
  210.3 0.5 fusion.17
  210.8 0.8 pad_maximum_fusion.1
  211.7 3.5 %all-to-all-start.3 = ((f32[64,16,128]{2,1,0:T(8,128)}), f32[64,16,128]{2,1,0:T(8,128)S(1)}, u32[]{:S(2)}, u32[]{:S(2)}) async-start(f32[64,16,128]{2,1,0:T(8,128)} %pad_maximum_fusion.1), calls=%async_computation.3 | async-start | bytes 1048576 | tf_op jit(solution)/shard_map/all_to_all | solution.py:45
  217.7 9.4 %psum.28 = f32[2]{0:T(128)S(1)} all-reduce(f32[2]{0:T(128)S(1)} %pad_maximum_fusion.15), channel_id=1, replica_groups=mesh['af'=4,'sa_0'=8,'sa_1'=4,'sa_2'=2] {'af'}, use_global_device_ids=true, to_apply=%region_4.5 | all-reduce | flops 2 | bytes 16 | tf_op jit(solution)/shard_map/psum | solution.py:51
  227.1 12.5 %psum.29 = f32[2]{0:T(128)S(1)} all-reduce(f32[2]{0:T(128)S(1)} %psum.28), channel_id=1, replica_groups=mesh['af'=4,'sa_0'=8,'sa_1'=4,'sa_2'=2] {'sa_0'}, use_global_device_ids=true, to_apply=%region_5.6 | all-reduce | flops 2 | bytes 16 | tf_op jit(solution)/shard_map/psum | solution.py:51
  239.6 7.3 %psum.30 = f32[2]{0:T(128)S(1)} all-reduce(f32[2]{0:T(128)S(1)} %psum.29), channel_id=1, replica_groups=mesh['af'=4,'sa_0'=8,'sa_1'=4,'sa_2'=2] {'sa_1'}, use_global_device_ids=true, to_apply=%region_6.7 | all-reduce | flops 2 | bytes 16 | tf_op jit(solution)/shard_map/psum | solution.py:51
  246.9 10.9 %psum.31 = f32[2]{0:T(128)S(1)} all-reduce(f32[2]{0:T(128)S(1)} %psum.30), channel_id=1, replica_groups=mesh['af'=4,'sa_0'=8,'sa_1'=4,'sa_2'=2] {'sa_2'}, use_global_device_ids=true, to_apply=%region_7.8 | all-reduce | flops 2 | bytes 16 | tf_op jit(solution)/shard_map/psum | solution.py:51
  257.8 0.5 broadcast_multiply_fusion
  258.3 0.3 copy.70
  258.9 0.8 fusion.158
  (54 shorter events, 1.2 us)
Async XLA Ops:
  7.2 114.0 %all-gather.2.cloned.1.call-start = ((), (), s32[]{:S(2)}) async-start(), calls=%async_computation.4 | async-start | bytes 17039360 | tf_op jit(solution)/shard_map/all_gather | solution.py:35
  10.9 120.3 %copy-start.1 = (f32[16,8,512]{2,1,0:T(8,128)S(1)}, f32[16,8,512]{2,1,0:T(8,128)}, u32[]{:S(2)}) copy-start(f32[16,8,512]{2,1,0:T(8,128)} %param.10) | copy-start | bytes 786436
  10.9 120.3 %copy-start.2 = (f32[16,8,512]{2,1,0:T(8,128)S(1)}, f32[16,8,512]{2,1,0:T(8,128)}, u32[]{:S(2)}) copy-start(f32[16,8,512]{2,1,0:T(8,128)} %param.11) | copy-start | bytes 786436
  10.9 120.3 %copy-start.3 = (bf16[16,8,512]{2,1,0:T(8,128)(2,1)S(1)}, bf16[16,8,512]{2,1,0:T(8,128)(2,1)}, u32[]{:S(2)}) copy-start(bf16[16,8,512]{2,1,0:T(8,128)(2,1)} %param.7) | copy-start | bytes 393220
  10.9 120.3 %copy-start.4 = (bf16[16,8,512]{2,1,0:T(8,128)(2,1)S(1)}, bf16[16,8,512]{2,1,0:T(8,128)(2,1)}, u32[]{:S(2)}) copy-start(bf16[16,8,512]{2,1,0:T(8,128)(2,1)} %param.6) | copy-start | bytes 393220
  11.0 120.3 %copy-start.5 = (f32[16]{0:T(128)S(1)}, f32[16]{0:T(128)}, u32[]{:S(2)}) copy-start(f32[16]{0:T(128)} %param.9) | copy-start | bytes 196
  11.0 120.3 %copy-start.6 = (f32[16]{0:T(128)S(1)}, f32[16]{0:T(128)}, u32[]{:S(2)}) copy-start(f32[16]{0:T(128)} %param.8) | copy-start | bytes 196
  121.1 11.0 %copy-start = (bf16[32,512,512]{2,1,0:T(8,128)(2,1)S(1)}, bf16[32,512,512]{2,1,0:T(8,128)(2,1)}, u32[]{:S(2)}) copy-start(bf16[32,512,512]{2,1,0:T(8,128)(2,1)} %all-gather.2.cloned.1.call-done) | copy-start | bytes 50331652
  137.0 11.1 %collective-permute-start = (f32[16,8,128]{2,1,0:T(8,128)S(1)}, f32[16,8,128]{2,1,0:T(8,128)S(1)}, u32[]{:S(2)}, u32[]{:S(2)}) collective-permute-start(f32[16,8,128]{2,1,0:T(8,128)S(1)} %get-tuple-element.29), channel_id=1, source_target_pairs={{0,64},{64,0},{128,192},{192,128},{1,65},{65,1},{129,193},{193,129... | collective-permute-start | bytes 196616 | tf_op jit(solution)/shard_map/ppermute | solution.py:28
  140.6 13.6 %all-to-all-start = ((f32[4,1,16384]{2,1,0:T(1,128)}), f32[4,1,16384]{2,1,0:T(1,128)S(1)}, u32[]{:S(2)}, u32[]{:S(2)}) async-start(f32[4,1,16384]{2,1,0:T(1,128)} %reshape.42), calls=%async_computation | async-start | bytes 524288 | tf_op jit(solution)/shard_map/all_to_all | solution.py:127
  144.3 7.3 %collective-permute-start.1 = (f32[16,8,128]{2,1,0:T(8,128)S(1)}, f32[16,8,128]{2,1,0:T(8,128)S(1)}, u32[]{:S(2)}, u32[]{:S(2)}) collective-permute-start(f32[16,8,128]{2,1,0:T(8,128)S(1)} %get-tuple-element.28), channel_id=1, source_target_pairs={{0,128},{64,192},{128,0},{192,64},{1,129},{65,193},{129,1},{193,65... | collective-permute-start | bytes 196616 | tf_op jit(solution)/shard_map/ppermute | solution.py:28
  147.3 7.0 %collective-permute-start.2 = (f32[16,8,128]{2,1,0:T(8,128)S(1)}, f32[16,8,128]{2,1,0:T(8,128)S(1)}, u32[]{:S(2)}, u32[]{:S(2)}) collective-permute-start(f32[16,8,128]{2,1,0:T(8,128)S(1)} %get-tuple-element.27), channel_id=1, source_target_pairs={{0,192},{64,128},{128,64},{192,0},{1,193},{65,129},{129,65},{193,1... | collective-permute-start | bytes 196616 | tf_op jit(solution)/shard_map/ppermute | solution.py:28
  158.5 25.3 %slice-start = ((s8[16777216]{0:T(1024)(128)(4,1)}), s8[4194304]{0:T(1024)(128)(4,1)S(1)}, s32[]{:S(2)}) async-start(s8[16777216]{0:T(1024)(128)(4,1)} %bitcast.67), calls=%async_computation.5 | async-start | bytes 8388608
  173.3 10.5 %slice-start.1 = ((s8[16777216]{0:T(1024)(128)(4,1)}), s8[4194304]{0:T(1024)(128)(4,1)S(1)}, s32[]{:S(2)}) async-start(s8[16777216]{0:T(1024)(128)(4,1)} %bitcast.67), calls=%async_computation.6 | async-start | bytes 8388608
  173.4 10.4 %slice-start.2 = ((s8[16777216]{0:T(1024)(128)(4,1)}), s8[4194304]{0:T(1024)(128)(4,1)S(1)}, s32[]{:S(2)}) async-start(s8[16777216]{0:T(1024)(128)(4,1)} %bitcast.67), calls=%async_computation.7 | async-start | bytes 8388608
  178.2 5.7 %slice-start.3 = ((s8[16777216]{0:T(1024)(128)(4,1)}), s8[4194304]{0:T(1024)(128)(4,1)S(1)}, s32[]{:S(2)}) async-start(s8[16777216]{0:T(1024)(128)(4,1)} %bitcast.67), calls=%async_computation.8 | async-start | bytes 8388608
  188.7 9.9 %collective-permute-start.3 = (f32[16,8,128]{2,1,0:T(8,128)S(1)}, f32[16,8,128]{2,1,0:T(8,128)S(1)}, u32[]{:S(2)}, u32[]{:S(2)}) collective-permute-start(f32[16,8,128]{2,1,0:T(8,128)S(1)} %get-tuple-element.25), channel_id=1, source_target_pairs={{0,64},{64,0},{128,192},{192,128},{1,65},{65,1},{129,193},{193,129... | collective-permute-start | bytes 196616 | tf_op jit(solution)/shard_map/ppermute | solution.py:28
  191.4 12.4 %all-to-all-start.2 = ((f32[4,1,16384]{2,1,0:T(1,128)}), f32[4,1,16384]{2,1,0:T(1,128)S(1)}, u32[]{:S(2)}, u32[]{:S(2)}) async-start(f32[4,1,16384]{2,1,0:T(1,128)} %reshape.44), calls=%async_computation.2 | async-start | bytes 524288 | tf_op jit(solution)/shard_map/all_to_all | solution.py:127
  194.8 6.2 %collective-permute-start.4 = (f32[16,8,128]{2,1,0:T(8,128)S(1)}, f32[16,8,128]{2,1,0:T(8,128)S(1)}, u32[]{:S(2)}, u32[]{:S(2)}) collective-permute-start(f32[16,8,128]{2,1,0:T(8,128)S(1)} %get-tuple-element.24), channel_id=1, source_target_pairs={{0,128},{64,192},{128,0},{192,64},{1,129},{65,193},{129,1},{193,65... | collective-permute-start | bytes 196616 | tf_op jit(solution)/shard_map/ppermute | solution.py:28
  197.7 6.1 %collective-permute-start.5 = (f32[16,8,128]{2,1,0:T(8,128)S(1)}, f32[16,8,128]{2,1,0:T(8,128)S(1)}, u32[]{:S(2)}, u32[]{:S(2)}) collective-permute-start(f32[16,8,128]{2,1,0:T(8,128)S(1)} %get-tuple-element.23), channel_id=1, source_target_pairs={{0,192},{64,128},{128,64},{192,0},{1,193},{65,129},{129,65},{193,1... | collective-permute-start | bytes 196616 | tf_op jit(solution)/shard_map/ppermute | solution.py:28
  211.7 46.7 %all-to-all-start.3 = ((f32[64,16,128]{2,1,0:T(8,128)}), f32[64,16,128]{2,1,0:T(8,128)S(1)}, u32[]{:S(2)}, u32[]{:S(2)}) async-start(f32[64,16,128]{2,1,0:T(8,128)} %pad_maximum_fusion.1), calls=%async_computation.3 | async-start | bytes 1048576 | tf_op jit(solution)/shard_map/all_to_all | solution.py:45
Sparse Core Ops, SparseCore 0:
  11.2 109.8 all-gather.1
